TPU v7x, 32 devices: a whole 2x2x4 slice. The times are simulated.
32 devices in a mesh: row: 8 (over z, core), col: 4 (over y, x).
Axes of the slice: x: 2, y: 2, z: 4, core: 2. Of those that a mesh axis runs over, the one named last changes fastest.
Arguments:
- act_codes: int32 [512, 7168], P('col', 'row'), may hold values from -127 to 127
- act_scales: float32 [512, 112], P('col', 'row'), may hold values from 0.005 to 0.03
- gate_weight: bfloat16 [7168, 18432], P('row', 'col'), may hold values from -0.0625 to 0.0625
- up_weight: bfloat16 [7168, 18432], P('row', 'col'), may hold values from -0.0625 to 0.0625
- down_weight: bfloat16 [18432, 7168], P('col', 'row'), may hold values from -0.046875 to 0.046875
Outputs:
- mixed: bfloat16 [512, 7168], P('col', 'row')
All inputs are finite; a program needn't handle non-finite values.
Results may differ from a plain program's by a relative error of at most 0.03.
Values may be sent and summed in bfloat16 or wider, within the bound.
A program may use at most 128 MiB of HBM per device.

v0:
```python
import jax
import jax.numpy as jnp
from jax import lax
from jax.sharding import PartitionSpec as P


def on_device(act_codes, act_scales, gate_weight, up_weight, down_weight):
    local_rows = act_codes.shape[0]
    width = act_codes.shape[1]
    nblocks = act_scales.shape[1]
    blocked = act_codes.astype(jnp.float32).reshape(local_rows, nblocks, width // nblocks)
    acts = (blocked * act_scales[:, :, None]).reshape(local_rows, width).astype(jnp.bfloat16)
    every = lax.all_gather(acts, "col", axis=0, tiled=True)
    hidden_width = gate_weight.shape[1]
    gate_part = jnp.dot(every, gate_weight, preferred_element_type=jnp.float32)
    up_part = jnp.dot(every, up_weight, preferred_element_type=jnp.float32)
    summed = lax.psum_scatter(
        jnp.concatenate([gate_part, up_part], axis=1).astype(jnp.bfloat16),
        "row",
        scatter_dimension=0,
        tiled=True,
    ).astype(jnp.float32)
    hidden = (jax.nn.silu(summed[:, :hidden_width]) * summed[:, hidden_width:]).astype(jnp.bfloat16)
    partial_value = jnp.dot(
        lax.all_gather(hidden, "row", axis=0, tiled=True),
        down_weight,
        preferred_element_type=jnp.float32,
    )
    mixed = lax.psum_scatter(
        partial_value.astype(jnp.bfloat16), "col", scatter_dimension=0, tiled=True
    )
    return mixed


def solution(mesh):
    placed = (P("col", "row"), P("col", "row"), P("row", "col"), P("row", "col"), P("col", "row"))
    return jax.shard_map(
        on_device, mesh=mesh, in_specs=placed, out_specs=P("col", "row"), check_vma=False
    )
```

profile of v0, /device:TPU:0, one launch (start us, length us, event | category | flops | bytes accessed | tf_op | source)
XLA Modules:
  0.0 236.7 jit_solution(11513722934624598675)
XLA Ops:
  6.5 0.0 reduce-scatter.3.cloned.1.call-start
  6.5 1.2 copy.7
  7.8 0.7 fusion.1
  8.5 0.0 slice-start
  8.5 14.2 %all_gather.6 = bf16[512,896]{0,1:T(8,128)(2,1)S(1)} all-gather(bf16[128,896]{0,1:T(8,128)(2,1)S(1)} %fusion.1), channel_id=1, replica_groups=mesh['row'=8,'col'=4] {'col'}, dimensions={0}, use_global_device_ids=true | all-gather | bytes 1146880 | tf_op jit(solution)/shard_map/all_gather | solution.py:13
  22.7 0.0 slice-start.1
  22.7 8.8 %convolution_convert_fusion = bf16[512,4608]{1,0:T(8,128)(2,1)S(1)} fusion(bf16[512,896]{0,1:T(8,128)(2,1)S(1)} %all_gather.6, bf16[896,4608]{1,0:T(8,128)(2,1)} %param.8), kind=kOutput, calls=%fused_computation.1 | convolution fusion | flops 4230217728 | bytes 13893632 | tf_op jit(solution)/shard_map/dot_general | solution.py:16
  31.5 0.0 slice-done
  31.5 0.0 slice-done.1
  31.6 5.4 %convolution_convert_fusion.1 = bf16[512,4608]{1,0:T(8,128)(2,1)S(1)} fusion(bf16[512,896]{0,1:T(8,128)(2,1)S(1)} %all_gather.6, bf16[896,4608]{1,0:T(8,128)(2,1)S(1)} %bitcast.11), kind=kOutput, calls=%fused_computation.2 | convolution fusion | flops 4230217728 | bytes 13893632 | tf_op jit(solution)/shard_map/dot_general | solution.py:15
  37.0 4.8 %pad_maximum_fusion = bf16[512,9216]{1,0:T(8,128)(2,1)} fusion(bf16[512,4608]{1,0:T(8,128)(2,1)S(1)} %convolution_convert_fusion, bf16[512,4608]{1,0:T(8,128)(2,1)S(1)} %convolution_convert_fusion.1), kind=kLoop, calls=%fused_computation | loop fusion | flops 18874368 | bytes 18874368 | tf_op jit(solution)/shard_map/concatenate | solution.py:18
  41.8 0.0 reduce-scatter.3.cloned.1.call-update
  41.8 0.0 all-gather.2.cloned.1.call-start
  41.9 99.8 %reduce-scatter.3.cloned.1.call-done = bf16[64,9216]{1,0:T(8,128)(2,1)} async-done(((bf16[512,9216]{1,0:T(8,128)(2,1)}), bf16[64,9216]{1,0:T(8,128)(2,1)}) %reduce-scatter.3.cloned.1.call-update) | async-done | bytes 1179664 | tf_op jit(solution)/shard_map/reduce_scatter | solution.py:17
  141.7 1.4 convert_element_type.18
  143.1 1.2 fusion
  144.3 0.0 all-gather.2.cloned.1.call-update
  144.3 0.0 reduce-scatter.5.cloned.1.call-start
  144.3 49.8 %all-gather.2.cloned.1.call-done = bf16[512,4608]{1,0:T(8,128)(2,1)} async-done(((bf16[64,4608]{1,0:T(8,128)(2,1)}), bf16[512,4608]{1,0:T(8,128)(2,1)}) %all-gather.2.cloned.1.call-update) | async-done | bytes 4718608 | tf_op jit(solution)/shard_map/all_gather | solution.py:25
  194.1 10.1 %convolution_convert_fusion.2 = bf16[512,896]{1,0:T(8,128)(2,1)} fusion(bf16[512,4608]{1,0:T(8,128)(2,1)} %all-gather.2.cloned.1.call-done, bf16[4608,896]{1,0:T(8,128)(2,1)} %param.9), kind=kOutput, calls=%fused_computation.3 | convolution fusion | flops 4228317184 | bytes 13893632 | tf_op jit(solution)/shard_map/dot_general | solution.py:24
  204.2 0.0 reduce-scatter.5.cloned.1.call-update
  204.2 26.0 %reduce-scatter.5.cloned.1.call-done = bf16[128,896]{1,0:T(8,128)(2,1)} async-done(((bf16[512,896]{1,0:T(8,128)(2,1)}), bf16[128,896]{1,0:T(8,128)(2,1)}) %reduce-scatter.5.cloned.1.call-update) | async-done | bytes 229392 | tf_op jit(solution)/shard_map/reduce_scatter | solution.py:29
  (1 shorter events, 0.0 us)
Async XLA Ops:
  6.5 135.2 %reduce-scatter.3.cloned.1.call-start = ((), (), s32[]{:S(2)}) async-start(), calls=%async_computation.2 | async-start | bytes 10616832 | tf_op jit(solution)/shard_map/reduce_scatter | solution.py:17
  8.5 23.0 %slice-start = ((s8[8257536]{0:T(1024)(128)(4,1)}), s8[4194304]{0:T(1024)(128)(4,1)S(1)}, s32[]{:S(2)}) async-start(s8[8257536]{0:T(1024)(128)(4,1)} %bitcast.10), calls=%async_computation.5 | async-start | bytes 8388608
  22.7 8.8 %slice-start.1 = ((s8[8257536]{0:T(1024)(128)(4,1)}), s8[4063232]{0:T(1024)(128)(4,1)S(1)}, s32[]{:S(2)}) async-start(s8[8257536]{0:T(1024)(128)(4,1)} %bitcast.10), calls=%async_computation.6 | async-start | bytes 8126464
  41.8 152.3 %all-gather.2.cloned.1.call-start = ((), (), s32[]{:S(2)}) async-start(), calls=%async_computation.3 | async-start | bytes 5308416 | tf_op jit(solution)/shard_map/all_gather | solution.py:25
  144.3 85.9 %reduce-scatter.5.cloned.1.call-start = ((), (), s32[]{:S(2)}) async-start(), calls=%async_computation.4 | async-start | bytes 1146880 | tf_op jit(solution)/shard_map/reduce_scatter | solution.py:29
Sparse Core Ops, SparseCore 0:
  41.9 99.7 reduce-scatter.2
  144.4 49.6 all-gather.1
  204.4 25.8 reduce-scatter.4
where the time goes:
time: 237 us
  waiting for transfers between devices  176 us (74%)
  matrix products  24.3 us (10%)
  blocking collectives  14.2 us (6%)
  between operations  13.2 us (6%)
  other arithmetic  8.09 us (3%)
    reduce_scatter x1, waiting for transfers between devices, on_device(): lax.psum_scatter(jnp.concatenate([gate_part, up_part], axis=1).astype(jnp...  99.8 us
    all_gather x1, waiting for transfers between devices, on_device(): lax.all_gather(hidden, 'row', axis=0, tiled=True)  49.8 us
    reduce_scatter x1, waiting for transfers between devices, on_device(): lax.psum_scatter(partial_value.astype(jnp.bfloat16), 'col', scatter_dimen...  26 us
    all_gather x1, blocking collectives, on_device(): every = lax.all_gather(acts, 'col', axis=0, tiled=True)  14.2 us
    dot_general x1, matrix products, on_device(): jnp.dot(lax.all_gather(hidden, 'row', axis=0, tiled=True), down_weight, p...  10.1 us
    dot_general x1, matrix products, on_device(): up_part = jnp.dot(every, up_weight, preferred_element_type=jnp.float32)  8.82 us
    dot_general x1, matrix products, on_device(): gate_part = jnp.dot(every, gate_weight, preferred_element_type=jnp.float32)  5.45 us
    concatenate x1, other arithmetic, on_device(): jnp.concatenate([gate_part, up_part], axis=1).astype(jnp.bfloat16)  4.77 us
  transfers between devices with their start and end apart: 3, of which 3 were waited for; matrix products, arithmetic and copies ran while one was open for 0% of the time, Pallas kernels for 0%

commit v1 on v0

--- a/solution.py
+++ b/solution.py
@@ -10,7 +10,14 @@
     nblocks = act_scales.shape[1]
     blocked = act_codes.astype(jnp.float32).reshape(local_rows, nblocks, width // nblocks)
     acts = (blocked * act_scales[:, :, None]).reshape(local_rows, width).astype(jnp.bfloat16)
-    every = lax.all_gather(acts, "col", axis=0, tiled=True)
+    n_dev = lax.axis_size("col")
+    route = [(i, (i + 1) % n_dev) for i in range(n_dev)]
+    parts = [acts]
+    for hop in range(1, n_dev):
+        parts = [lax.ppermute(parts[0], "col", route), *parts]
+    full = jnp.concatenate(parts, axis=0)
+    turn = (lax.axis_index("col") + 1) * parts[-1].shape[0]
+    every = jnp.roll(full, turn, axis=0)
     hidden_width = gate_weight.shape[1]
     gate_part = jnp.dot(every, gate_weight, preferred_element_type=jnp.float32)
     up_part = jnp.dot(every, up_weight, preferred_element_type=jnp.float32)

time: 237 us -> 248 us (1.046)
  waiting for transfers between devices: 176 us -> 196 us
  blocking collectives: 14.2 us -> 0 us
  starting transfers between devices: 0.09 us -> 3.89 us
    ppermute x0 -> x3, waiting for transfers between devices: none -> 20.4 us  [on_device(): parts = [lax.ppermute(parts[0], 'col', route), *parts]]
    all_gather x1 -> x0, blocking collectives: 14.2 us -> none  [on_device(): every = lax.all_gather(acts, 'col', axis=0, tiled=True)]
    ppermute x0 -> x3, starting transfers between devices: none -> 3.81 us  [on_device(): parts = [lax.ppermute(parts[0], 'col', route), *parts]]
  transfers between devices with their start and end apart: 3 -> 6, of which waited for: 3 -> 6; matrix products, arithmetic and copies ran while one was open for 0% -> 0% of each run, Pallas kernels for 0% -> 0%
where the time goes in v1:
time: 248 us; the launch traced here: 247 us
  waiting for transfers between devices  196 us (79%)
  matrix products  24.4 us (10%)
  between operations  13.2 us (5%)
  other arithmetic  8.14 us (3%)
  starting transfers between devices  3.89 us (2%)
    reduce_scatter x1, waiting for transfers between devices, on_device(): lax.psum_scatter(jnp.concatenate([gate_part, up_part], axis=1).astype(jnp...  99.8 us
    all_gather x1, waiting for transfers between devices, on_device(): lax.all_gather(hidden, 'row', axis=0, tiled=True)  49.8 us
    reduce_scatter x1, waiting for transfers between devices, on_device(): lax.psum_scatter(partial_value.astype(jnp.bfloat16), 'col', scatter_dimen...  26 us
    ppermute x3, waiting for transfers between devices, on_device(): parts = [lax.ppermute(parts[0], 'col', route), *parts]  20.4 us
    dot_general x1, matrix products, on_device(): jnp.dot(lax.all_gather(hidden, 'row', axis=0, tiled=True), down_weight, p...  10.1 us
    dot_general x1, matrix products, on_device(): up_part = jnp.dot(every, up_weight, preferred_element_type=jnp.float32)  8.85 us
    dot_general x1, matrix products, on_device(): gate_part = jnp.dot(every, gate_weight, preferred_element_type=jnp.float32)  5.48 us
  transfers between devices with their start and end apart: 6, of which 6 were waited for; matrix products, arithmetic and copies ran while one was open for 0% of the time, Pallas kernels for 0%

profile of v1, /device:TPU:0, one launch (start us, length us, event | category | flops | bytes accessed | tf_op | source)
XLA Modules:
  0.0 247.4 jit_solution(10797811361236191859)
XLA Ops:
  6.5 0.0 reduce-scatter.3.cloned.1.call-start
  6.5 1.2 copy.7
  7.8 0.7 fusion.3
  8.5 3.0 %collective-permute-start = (bf16[128,896]{0,1:T(8,128)(2,1)S(1)}, bf16[128,896]{0,1:T(8,128)(2,1)S(1)}, u32[]{:S(2)}, u32[]{:S(2)}) collective-permute-start(bf16[128,896]{0,1:T(8,128)(2,1)S(1)} %fusion.3), channel_id=1, source_target_pairs={{0,1},{1,2},{2,3},{3,0},{4,5},{5,6},{6,7},{7,4},{8,9},{9,10},{10,1... | collective-permute-start | bytes 688136 | tf_op jit(solution)/shard_map/ppermute | solution.py:17
  11.5 6.6 %collective-permute-done = bf16[128,896]{0,1:T(8,128)(2,1)S(1)} collective-permute-done((bf16[128,896]{0,1:T(8,128)(2,1)S(1)}, bf16[128,896]{0,1:T(8,128)(2,1)S(1)}, u32[]{:S(2)}, u32[]{:S(2)}) %collective-permute-start) | collective-permute-done | bytes 229408 | tf_op jit(solution)/shard_map/ppermute | solution.py:17
  18.1 0.8 collective-permute-start.1
  18.9 6.9 %collective-permute-done.1 = bf16[128,896]{0,1:T(8,128)(2,1)S(1)} collective-permute-done((bf16[128,896]{0,1:T(8,128)(2,1)S(1)}, bf16[128,896]{0,1:T(8,128)(2,1)S(1)}, u32[]{:S(2)}, u32[]{:S(2)}) %collective-permute-start.1) | collective-permute-done | bytes 229408 | tf_op jit(solution)/shard_map/ppermute | solution.py:17
  25.8 0.0 collective-permute-start.2
  25.8 6.9 %collective-permute-done.2 = bf16[128,896]{0,1:T(8,128)(2,1)S(1)} collective-permute-done((bf16[128,896]{0,1:T(8,128)(2,1)S(1)}, bf16[128,896]{0,1:T(8,128)(2,1)S(1)}, u32[]{:S(2)}, u32[]{:S(2)}) %collective-permute-start.2) | collective-permute-done | bytes 229408 | tf_op jit(solution)/shard_map/ppermute | solution.py:17
  32.7 0.1 constant_dynamic-update-slice_fusion.7
  32.7 0.1 constant_dynamic-update-slice_fusion.6
  32.8 0.1 constant_dynamic-update-slice_fusion.5
  32.9 0.1 constant_dynamic-update-slice_fusion.4
  33.0 0.1 constant_dynamic-update-slice_fusion.3
  33.1 0.1 constant_dynamic-update-slice_fusion.2
  33.1 0.1 constant_dynamic-update-slice_fusion.1
  33.2 0.0 slice-start
  33.2 0.1 constant_dynamic-update-slice_fusion
  33.3 0.0 slice-start.1
  33.3 8.9 %convolution_convert_fusion = bf16[512,4608]{1,0:T(8,128)(2,1)S(1)} fusion(bf16[896,4608]{1,0:T(8,128)(2,1)} %param.8, bf16[1024,896]{0,1:T(8,128)(2,1)S(1)} %constant_dynamic-update-slice_fusion, s32[]{:T(128)S(6)} %select_n.14), kind=kOutput, calls=%fused_computation.1 | convolution fusion | flops 4230217728 | bytes 13893636 | tf_op jit(solution)/shard_map/dot_general | solution.py:23
  42.2 0.0 slice-done
  42.2 0.0 slice-done.1
  42.2 5.5 %convolution_convert_fusion.1 = bf16[512,4608]{1,0:T(8,128)(2,1)S(1)} fusion(bf16[896,4608]{1,0:T(8,128)(2,1)S(1)} %bitcast.9, bf16[1024,896]{0,1:T(8,128)(2,1)S(1)} %constant_dynamic-update-slice_fusion, s32[]{:T(128)S(6)} %select_n.14), kind=kOutput, calls=%fused_computation.2 | convolution fusion | flops 4230217728 | bytes 13893636 | tf_op jit(solution)/shard_map/dot_general | solution.py:22
  47.7 4.8 %pad_maximum_fusion = bf16[512,9216]{1,0:T(8,128)(2,1)} fusion(bf16[512,4608]{1,0:T(8,128)(2,1)S(1)} %convolution_convert_fusion, bf16[512,4608]{1,0:T(8,128)(2,1)S(1)} %convolution_convert_fusion.1), kind=kLoop, calls=%fused_computation | loop fusion | flops 18874368 | bytes 18874368 | tf_op jit(solution)/shard_map/concatenate | solution.py:25
  52.5 0.0 reduce-scatter.3.cloned.1.call-update
  52.5 0.0 all-gather.2.cloned.1.call-start
  52.6 99.8 %reduce-scatter.3.cloned.1.call-done = bf16[64,9216]{1,0:T(8,128)(2,1)} async-done(((bf16[512,9216]{1,0:T(8,128)(2,1)}), bf16[64,9216]{1,0:T(8,128)(2,1)}) %reduce-scatter.3.cloned.1.call-update) | async-done | bytes 1179664 | tf_op jit(solution)/shard_map/reduce_scatter | solution.py:24
  152.4 1.4 convert_element_type.18
  153.8 1.2 fusion
  154.9 0.0 all-gather.2.cloned.1.call-update
  155.0 0.0 reduce-scatter.5.cloned.1.call-start
  155.0 49.8 %all-gather.2.cloned.1.call-done = bf16[512,4608]{1,0:T(8,128)(2,1)} async-done(((bf16[64,4608]{1,0:T(8,128)(2,1)}), bf16[512,4608]{1,0:T(8,128)(2,1)}) %all-gather.2.cloned.1.call-update) | async-done | bytes 4718608 | tf_op jit(solution)/shard_map/all_gather | solution.py:32
  204.8 10.1 %convolution_convert_fusion.2 = bf16[512,896]{1,0:T(8,128)(2,1)} fusion(bf16[512,4608]{1,0:T(8,128)(2,1)} %all-gather.2.cloned.1.call-done, bf16[4608,896]{1,0:T(8,128)(2,1)} %param.9), kind=kOutput, calls=%fused_computation.3 | convolution fusion | flops 4228317184 | bytes 13893632 | tf_op jit(solution)/shard_map/dot_general | solution.py:31
  214.9 0.0 reduce-scatter.5.cloned.1.call-update
  214.9 26.0 %reduce-scatter.5.cloned.1.call-done = bf16[128,896]{1,0:T(8,128)(2,1)} async-done(((bf16[512,896]{1,0:T(8,128)(2,1)}), bf16[128,896]{1,0:T(8,128)(2,1)}) %reduce-scatter.5.cloned.1.call-update) | async-done | bytes 229392 | tf_op jit(solution)/shard_map/reduce_scatter | solution.py:36
  (1 shorter events, 0.0 us)
Async XLA Ops:
  6.5 145.8 %reduce-scatter.3.cloned.1.call-start = ((), (), s32[]{:S(2)}) async-start(), calls=%async_computation.2 | async-start | bytes 10616832 | tf_op jit(solution)/shard_map/reduce_scatter | solution.py:24
  8.5 9.6 %collective-permute-start = (bf16[128,896]{0,1:T(8,128)(2,1)S(1)}, bf16[128,896]{0,1:T(8,128)(2,1)S(1)}, u32[]{:S(2)}, u32[]{:S(2)}) collective-permute-start(bf16[128,896]{0,1:T(8,128)(2,1)S(1)} %fusion.3), channel_id=1, source_target_pairs={{0,1},{1,2},{2,3},{3,0},{4,5},{5,6},{6,7},{7,4},{8,9},{9,10},{10,1... | collective-permute-start | bytes 688136 | tf_op jit(solution)/shard_map/ppermute | solution.py:17
  18.1 7.7 %collective-permute-start.1 = (bf16[128,896]{0,1:T(8,128)(2,1)S(1)}, bf16[128,896]{0,1:T(8,128)(2,1)S(1)}, u32[]{:S(2)}, u32[]{:S(2)}) collective-permute-start(bf16[128,896]{0,1:T(8,128)(2,1)S(1)} %collective-permute-done), channel_id=1, source_target_pairs={{0,1},{1,2},{2,3},{3,0},{4,5},{5,6},{6,7},{7,4},{8,9},{9,10},{10,1... | collective-permute-start | bytes 688136 | tf_op jit(solution)/shard_map/ppermute | solution.py:17
  25.8 6.9 %collective-permute-start.2 = (bf16[128,896]{0,1:T(8,128)(2,1)S(1)}, bf16[128,896]{0,1:T(8,128)(2,1)S(1)}, u32[]{:S(2)}, u32[]{:S(2)}) collective-permute-start(bf16[128,896]{0,1:T(8,128)(2,1)S(1)} %collective-permute-done.1), channel_id=1, source_target_pairs={{0,1},{1,2},{2,3},{3,0},{4,5},{5,6},{6,7},{7,4},{8,9},{9,10},{10,1... | collective-permute-start | bytes 688136 | tf_op jit(solution)/shard_map/ppermute | solution.py:17
  33.2 9.0 %slice-start = ((s8[8257536]{0:T(1024)(128)(4,1)}), s8[4194304]{0:T(1024)(128)(4,1)S(1)}, s32[]{:S(2)}) async-start(s8[8257536]{0:T(1024)(128)(4,1)} %bitcast.8), calls=%async_computation.5 | async-start | bytes 8388608
  33.3 8.9 %slice-start.1 = ((s8[8257536]{0:T(1024)(128)(4,1)}), s8[4063232]{0:T(1024)(128)(4,1)S(1)}, s32[]{:S(2)}) async-start(s8[8257536]{0:T(1024)(128)(4,1)} %bitcast.8), calls=%async_computation.6 | async-start | bytes 8126464
  52.5 152.2 %all-gather.2.cloned.1.call-start = ((), (), s32[]{:S(2)}) async-start(), calls=%async_computation.3 | async-start | bytes 5308416 | tf_op jit(solution)/shard_map/all_gather | solution.py:32
  155.0 85.9 %reduce-scatter.5.cloned.1.call-start = ((), (), s32[]{:S(2)}) async-start(), calls=%async_computation.4 | async-start | bytes 1146880 | tf_op jit(solution)/shard_map/reduce_scatter | solution.py:36
Sparse Core Ops, SparseCore 0:
  52.7 99.6 reduce-scatter.2
  155.1 49.6 all-gather.1
  215.0 25.8 reduce-scatter.4
